TPU v7x, 32 devices: a whole 2x2x4 slice. The times are simulated.
32 devices in a mesh: batch: 16 (over z, y, core), gene: 2 (over x).
Axes of the slice: x: 2, y: 2, z: 4, core: 2. Of those that a mesh axis runs over, the one named last changes fastest.
Arguments:
- umi_counts: int32 [16384, 8192], P('batch', 'gene'), may hold values from 0 to 65535
- cell_donors: int32 [16384], P('batch'), may hold values from 0 to 127
- cell_types: int32 [16384], P('batch'), may hold values from 0 to 23
- live_cells: int32 [16], P('batch'), may hold values from 1 to 1024, 10240 in all
- dosages: int32 [128, 2048], P(None, 'batch'), may hold values from 0 to 2
Outputs:
- scores: bfloat16 [24, 8192, 2048], P(None, ('gene', 'batch'))
All inputs are finite; a program needn't handle non-finite values. No bound on the sum of `live_cells` on one device may be relied on, other than what follows from the above.
Results may differ from a plain program's by a relative error of at most 0.0069.
Values may be sent and summed in bfloat16 or wider, within the bound.
A program may use at most 128 MiB of HBM per device.

v0:
```python
import jax
import jax.numpy as jnp
from jax import lax
from jax.sharding import PartitionSpec as P

TYPES = 24
DONORS = 128


def one_hot_rows(group_ids, total_groups):
    columns = jnp.arange(total_groups, dtype=jnp.int32)
    return (group_ids[:, None] == columns[None, :]).astype(jnp.bfloat16)


def standardize_dosage(block_dosage):
    genotype = block_dosage.astype(jnp.float32)
    centred = genotype - jnp.mean(genotype, axis=0, keepdims=True)
    return (centred * lax.rsqrt(jnp.mean(centred * centred, axis=0, keepdims=True) + 1e-06)).astype(
        jnp.bfloat16
    )


def on_device(umi_counts, cell_donors, cell_types, live_cells, dosages):
    total_groups = TYPES * DONORS
    cell_slots = umi_counts.shape[0]
    genes_block = umi_counts.shape[1]
    batch_count = lax.axis_size("batch")
    genes_local = genes_block // batch_count
    slot_index = jnp.arange(cell_slots, dtype=jnp.int32)
    alive_mask = slot_index < live_cells[0]
    cell_group = jnp.where(alive_mask, cell_types * DONORS + cell_donors, -1)
    rounded = umi_counts.astype(jnp.bfloat16)
    exchanged = lax.all_to_all(rounded, "batch", split_axis=1, concat_axis=0, tiled=True)
    all_groups = lax.all_gather(cell_group, "batch", axis=0, tiled=True)
    block_rows = 4 * cell_slots
    block_turns = batch_count // 4

    def add_block(step_index, totals):
        block_counts = lax.dynamic_slice_in_dim(exchanged, step_index * block_rows, block_rows, 0)
        block_groups = lax.dynamic_slice_in_dim(all_groups, step_index * block_rows, block_rows, 0)
        table = one_hot_rows(block_groups, total_groups)
        return totals + lax.dot_general(
            block_counts, table, (((0,), (0,)), ((), ())), preferred_element_type=jnp.float32
        )

    pseudo = lax.fori_loop(
        0, block_turns, add_block, jnp.zeros((genes_local, total_groups), jnp.float32)
    )
    partial_library = jnp.sum(pseudo, axis=0)
    library = jnp.maximum(lax.psum(partial_library, ("batch", "gene")), 1.0)
    logged = jnp.log1p(10000.0 * pseudo / library[None, :]).reshape(genes_local, TYPES, DONORS)
    centred = logged - jnp.mean(logged, axis=2, keepdims=True)
    standard = (
        centred * lax.rsqrt(jnp.mean(centred * centred, axis=2, keepdims=True) + 1e-06)
    ).astype(jnp.bfloat16)
    standard_rows = jnp.transpose(standard, (1, 0, 2)).reshape(TYPES * genes_local, DONORS)
    factor = DONORS ** (-0.5)
    geno_local = standardize_dosage(dosages)
    geno_piece = lax.all_gather(geno_local, "batch", axis=1, tiled=True)
    product = jnp.dot(standard_rows, geno_piece, preferred_element_type=jnp.float32) * factor
    return product.reshape(TYPES, genes_local, geno_piece.shape[1]).astype(jnp.bfloat16)


def solution(mesh):
    placed = (P("batch", "gene"), P("batch"), P("batch"), P("batch"), P(None, "batch"))
    return jax.shard_map(
        on_device,
        mesh=mesh,
        in_specs=placed,
        out_specs=P(None, ("gene", "batch"), None),
        check_vma=False,
    )
```

profile of v0, /device:TPU:14, one launch (start us, length us, event | category | flops | bytes accessed | tf_op | source)
XLA Modules:
  0.0 357.4 jit_solution(3607183109049914522)
XLA Ops:
  0.0 9.0 %convert_element_type.21 = bf16[1024,4096]{1,0:T(8,128)(2,1)} convert(s32[1024,4096]{1,0:T(8,128)} %param.7) | non-fusion elementwise | flops 4194304 | bytes 25165824 | tf_op jit(solution)/shard_map/convert_element_type | solution.py:32
  9.0 7.4 %copy.16 = bf16[128,16,8,256]{3,2,0,1:T(8,128)(2,1)} copy(bf16[128,16,8,256]{3,2,1,0:T(8,128)(2,1)} %bitcast.19) | data formatting | bytes 16777216 | tf_op jit(solution)/shard_map/all_to_all | solution.py:33
  16.5 6.4 %all-to-all-start = ((bf16[1024,16,256]{2,0,1:T(8,128)(2,1)}), bf16[1024,16,256]{2,0,1:T(8,128)(2,1)}, u32[]{:S(2)}, u32[]{:S(2)}) async-start(bf16[1024,16,256]{2,0,1:T(8,128)(2,1)} %bitcast.20), calls=%async_computation | async-start | bytes 16777216 | tf_op jit(solution)/shard_map/all_to_all | solution.py:33
  23.5 0.0 copy-done.2
  23.5 0.0 copy-done.3
  23.5 191.0 %all_gather.6 = s32[16384]{0:T(1024)S(1)} all-gather(s32[1024]{0:T(1024)S(1)} %add_select_fusion), channel_id=1, replica_groups=mesh['batch'=16,'gene'=2] {'batch'}, dimensions={0}, use_global_device_ids=true | all-gather | bytes 69632 | tf_op jit(solution)/shard_map/all_gather | solution.py:34
  214.5 0.0 copy-done.1
  214.6 18.3 %all_gather.7 = bf16[128,2048]{1,0:T(8,128)(2,1)} all-gather(bf16[128,128]{1,0:T(8,128)(2,1)S(1)} %multiply_convert_fusion.2), channel_id=1, replica_groups=mesh['batch'=16,'gene'=2] {'batch'}, dimensions={1}, use_global_device_ids=true | all-gather | bytes 557056 | tf_op jit(solution)/shard_map/all_gather | solution.py:59
  232.9 0.0 all-to-all-done
  232.9 57.8 %while.14 = (s32[]{:T(128)}, f32[256,3072]{1,0:T(8,128)S(1)}, bf16[16384,256]{1,0:T(8,128)(2,1)}, s32[16384]{0:T(1024)S(1)}, s32[]{:T(128)}, /*index=5*/s32[]{:T(128)}, s32[]{:T(128)}, s32[]{:T(128)}) while((s32[]{:T(128)}, f32[256,3072]{1,0:T(8,128)S(1)}, bf16[16384,256]{1,0:T(8,128)(2,1)}, s32[16384]{0:T(1024)S(1)}, s32[]{:T(128)}, ...), condition=%wide.region_1.2_spmd.clone, body=%wide.region_0.1_spmd.clone.sunk | while | flops 6456606720 | bytes 8437917 | solution.py:46
  232.9 14.4 %fusion.11 = f32[256,3072]{1,0:T(8,128)S(1)} fusion(s32[4096]{0:T(1024)S(1)} %dynamic_slice.21, f32[256,3072]{1,0:T(8,128)S(1)} %get-tuple-element.142, bf16[16384,256]{1,0:T(8,128)(2,1)} %get-tuple-element.151, s32[]{:T(128)S(6)} %select_n.16, pred[]{:T(512)S(6)} %compare.3), kind=kOutput, calls=%fused_computation.3.clone.1 | convolution fusion | flops 6456606720 | bytes 8404997 | tf_op jit(solution)/shard_map/while/body/eval_jaxpr/dot_general | solution.py:42
  247.4 14.4 %fusion.11 = f32[256,3072]{1,0:T(8,128)S(1)} fusion(s32[4096]{0:T(1024)S(1)} %dynamic_slice.21, f32[256,3072]{1,0:T(8,128)S(1)} %get-tuple-element.142, bf16[16384,256]{1,0:T(8,128)(2,1)} %get-tuple-element.151, s32[]{:T(128)S(6)} %select_n.16, pred[]{:T(512)S(6)} %compare.3), kind=kOutput, calls=%fused_computation.3.clone.1 | convolution fusion | flops 6456606720 | bytes 8404997 | tf_op jit(solution)/shard_map/while/body/eval_jaxpr/dot_general | solution.py:42
  261.8 14.4 %fusion.11 = f32[256,3072]{1,0:T(8,128)S(1)} fusion(s32[4096]{0:T(1024)S(1)} %dynamic_slice.21, f32[256,3072]{1,0:T(8,128)S(1)} %get-tuple-element.142, bf16[16384,256]{1,0:T(8,128)(2,1)} %get-tuple-element.151, s32[]{:T(128)S(6)} %select_n.16, pred[]{:T(512)S(6)} %compare.3), kind=kOutput, calls=%fused_computation.3.clone.1 | convolution fusion | flops 6456606720 | bytes 8404997 | tf_op jit(solution)/shard_map/while/body/eval_jaxpr/dot_general | solution.py:42
  276.3 14.4 %fusion.11 = f32[256,3072]{1,0:T(8,128)S(1)} fusion(s32[4096]{0:T(1024)S(1)} %dynamic_slice.21, f32[256,3072]{1,0:T(8,128)S(1)} %get-tuple-element.142, bf16[16384,256]{1,0:T(8,128)(2,1)} %get-tuple-element.151, s32[]{:T(128)S(6)} %select_n.16, pred[]{:T(512)S(6)} %compare.3), kind=kOutput, calls=%fused_computation.3.clone.1 | convolution fusion | flops 6456606720 | bytes 8404997 | tf_op jit(solution)/shard_map/while/body/eval_jaxpr/dot_general | solution.py:42
  290.7 2.5 copy.12
  293.3 0.2 reduce_sum.45
  293.4 44.2 %psum.7 = f32[3072]{0:T(1024)S(1)} all-reduce(f32[3072]{0:T(1024)S(1)} %reduce_sum.45), channel_id=1, replica_groups=mesh['batch'=16,'gene'=2] {'batch','gene'}, use_global_device_ids=true, to_apply=%region_3.4 | all-reduce | flops 3072 | bytes 24576 | tf_op jit(solution)/shard_map/psum | solution.py:50
  337.7 3.1 divide_log-plus-one_fusion
  340.8 0.2 reduce_sum.46
  341.1 0.4 multiply_reduce_fusion
  341.5 1.6 fusion.5
  343.1 2.0 copy.13
  345.0 0.0 copy-done
  345.0 12.4 %multiply_convert_fusion = bf16[6144,2048]{1,0:T(8,128)(2,1)} fusion(bf16[6144,128]{1,0:T(8,128)(2,1)S(1)} %bitcast.21, bf16[128,2048]{1,0:T(8,128)(2,1)S(1)} %copy-done), kind=kOutput, calls=%fused_computation.6 | convolution fusion | flops 3246391296 | bytes 27262976 | tf_op jit(solution)/shard_map/dot_general | solution.py:60
  (18 shorter events, 0.2 us)
Async XLA Ops:
  16.5 7.0 %copy-start.2 = (s32[1024]{0:T(1024)S(1)}, s32[1024]{0:T(1024)}, u32[]{:S(2)}) copy-start(s32[1024]{0:T(1024)} %param.8) | copy-start | bytes 12292
  16.5 7.0 %copy-start.3 = (s32[1024]{0:T(1024)S(1)}, s32[1024]{0:T(1024)}, u32[]{:S(2)}) copy-start(s32[1024]{0:T(1024)} %param.9) | copy-start | bytes 12292
  16.5 198.0 %copy-start.1 = (s32[128,128]{1,0:T(8,128)S(1)}, s32[128,128]{1,0:T(8,128)}, u32[]{:S(2)}) copy-start(s32[128,128]{1,0:T(8,128)} %param.11) | copy-start | bytes 196612
  16.5 216.4 %all-to-all-start = ((bf16[1024,16,256]{2,0,1:T(8,128)(2,1)}), bf16[1024,16,256]{2,0,1:T(8,128)(2,1)}, u32[]{:S(2)}, u32[]{:S(2)}) async-start(bf16[1024,16,256]{2,0,1:T(8,128)(2,1)} %bitcast.20), calls=%async_computation | async-start | bytes 16777216 | tf_op jit(solution)/shard_map/all_to_all | solution.py:33
  343.1 2.0 copy-start
where the time goes:
time: 358 us; the launch traced here: 357 us
  blocking collectives  253 us (71%)
  matrix products  70 us (20%)
  other arithmetic  14.7 us (4%)
  local copies, waits for them, and re-layouts  12 us (3%)
  starting transfers between devices  6.37 us (2%)
    all_gather x1, blocking collectives, on_device(): all_groups = lax.all_gather(cell_group, 'batch', axis=0, tiled=True)  191 us
    dot_general x4, matrix products, add_block(): lax.dot_general(block_counts, table, (((0,), (0,)), ((), ())), preferred_...  57.6 us
    psum x1, blocking collectives, on_device(): library = jnp.maximum(lax.psum(partial_library, ('batch', 'gene')), 1.0)  44.2 us
    all_gather x1, blocking collectives, on_device(): geno_piece = lax.all_gather(geno_local, 'batch', axis=1, tiled=True)  18.3 us
    dot_general x1, matrix products, on_device(): jnp.dot(standard_rows, geno_piece, preferred_element_type=jnp.float32)  12.4 us
    convert_element_type x1, other arithmetic, on_device(): rounded = umi_counts.astype(jnp.bfloat16)  9.05 us
    all_to_all x1, local copies, waits for them, and re-layouts, on_device(): lax.all_to_all(rounded, 'batch', split_axis=1, concat_axis=0, tiled=True)  7.43 us
  transfers between devices with their start and end apart: 1, of which 0 were waited for; matrix products, arithmetic and copies ran while one was open for 0% of the time, Pallas kernels for 0%

commit v1 on v0

--- a/solution.py
+++ b/solution.py
@@ -47,7 +47,7 @@
         0, block_turns, add_block, jnp.zeros((genes_local, total_groups), jnp.float32)
     )
     partial_library = jnp.sum(pseudo, axis=0)
-    library = jnp.maximum(lax.psum(partial_library, ("batch", "gene")), 1.0)
+    library = jnp.maximum(jnp.sum(lax.all_gather(partial_library, ("batch", "gene")), axis=0), 1.0)
     logged = jnp.log1p(10000.0 * pseudo / library[None, :]).reshape(genes_local, TYPES, DONORS)
     centred = logged - jnp.mean(logged, axis=2, keepdims=True)
     standard = (

time: 358 us -> 387 us (1.081)
  the two profiles are of different devices: /device:TPU:14 before, /device:TPU:0 now
where the time goes in v1:
time: 387 us
  blocking collectives  282 us (73%)
  matrix products  70 us (18%)
  other arithmetic  14.7 us (4%)
  local copies, waits for them, and re-layouts  12.1 us (3%)
  starting transfers between devices  7.6 us (2%)
    all_gather x1, blocking collectives, on_device(): all_groups = lax.all_gather(cell_group, 'batch', axis=0, tiled=True)  151 us
    all_gather x1, blocking collectives, on_device(): lax.all_gather(partial_library, ('batch', 'gene'))  67 us
    all_gather x1, blocking collectives, on_device(): geno_piece = lax.all_gather(geno_local, 'batch', axis=1, tiled=True)  63.4 us
    dot_general x4, matrix products, add_block(): lax.dot_general(block_counts, table, (((0,), (0,)), ((), ())), preferred_...  57.6 us
    dot_general x1, matrix products, on_device(): jnp.dot(standard_rows, geno_piece, preferred_element_type=jnp.float32)  12.4 us
    convert_element_type x1, other arithmetic, on_device(): rounded = umi_counts.astype(jnp.bfloat16)  9.05 us
  transfers between devices with their start and end apart: 1, of which 0 were waited for; matrix products, arithmetic and copies ran while one was open for 0% of the time, Pallas kernels for 0%

profile of v1, /device:TPU:0, one launch (start us, length us, event | category | flops | bytes accessed | tf_op | source)
XLA Modules:
  0.0 386.9 jit_solution(691277206863017395)
XLA Ops:
  0.0 9.0 %convert_element_type.21 = bf16[1024,4096]{1,0:T(8,128)(2,1)} convert(s32[1024,4096]{1,0:T(8,128)} %param.7) | non-fusion elementwise | flops 4194304 | bytes 25165824 | tf_op jit(solution)/shard_map/convert_element_type | solution.py:32
  9.0 7.4 %copy.19 = bf16[128,16,8,256]{3,2,0,1:T(8,128)(2,1)} copy(bf16[128,16,8,256]{3,2,1,0:T(8,128)(2,1)} %bitcast.19) | data formatting | bytes 16777216 | tf_op jit(solution)/shard_map/all_to_all | solution.py:33
  16.5 7.6 %all-to-all-start = ((bf16[1024,16,256]{2,0,1:T(8,128)(2,1)}), bf16[1024,16,256]{2,0,1:T(8,128)(2,1)}, u32[]{:S(2)}, u32[]{:S(2)}) async-start(bf16[1024,16,256]{2,0,1:T(8,128)(2,1)} %bitcast.20), calls=%async_computation | async-start | bytes 16777216 | tf_op jit(solution)/shard_map/all_to_all | solution.py:33
  24.7 0.0 copy-done.2
  24.8 0.0 copy-done.3
  24.8 151.2 %all_gather.12 = s32[16384]{0:T(1024)S(1)} all-gather(s32[1024]{0:T(1024)S(1)} %add_select_fusion), channel_id=1, replica_groups=mesh['batch'=16,'gene'=2] {'batch'}, dimensions={0}, use_global_device_ids=true | all-gather | bytes 69632 | tf_op jit(solution)/shard_map/all_gather | solution.py:34
  176.0 0.0 copy-done.1
  176.1 63.4 %all_gather.15 = bf16[128,2048]{1,0:T(8,128)(2,1)} all-gather(bf16[128,128]{1,0:T(8,128)(2,1)S(1)} %multiply_convert_fusion.2), channel_id=1, replica_groups=mesh['batch'=16,'gene'=2] {'batch'}, dimensions={1}, use_global_device_ids=true | all-gather | bytes 557056 | tf_op jit(solution)/shard_map/all_gather | solution.py:59
  239.6 0.0 all-to-all-done
  239.6 57.8 %while.14 = (s32[]{:T(128)}, f32[256,3072]{1,0:T(8,128)S(1)}, bf16[16384,256]{1,0:T(8,128)(2,1)}, s32[16384]{0:T(1024)S(1)}, s32[]{:T(128)}, /*index=5*/s32[]{:T(128)}, s32[]{:T(128)}, s32[]{:T(128)}) while((s32[]{:T(128)}, f32[256,3072]{1,0:T(8,128)S(1)}, bf16[16384,256]{1,0:T(8,128)(2,1)}, s32[16384]{0:T(1024)S(1)}, s32[]{:T(128)}, ...), condition=%wide.region_1.2_spmd.clone, body=%wide.region_0.1_spmd.clone.sunk | while | flops 6456606720 | bytes 8437917 | solution.py:46
  239.6 14.4 %fusion.11 = f32[256,3072]{1,0:T(8,128)S(1)} fusion(s32[4096]{0:T(1024)S(1)} %dynamic_slice.21, f32[256,3072]{1,0:T(8,128)S(1)} %get-tuple-element.142, bf16[16384,256]{1,0:T(8,128)(2,1)} %get-tuple-element.151, s32[]{:T(128)S(6)} %select_n.16, pred[]{:T(512)S(6)} %compare.3), kind=kOutput, calls=%fused_computation.3.clone.1 | convolution fusion | flops 6456606720 | bytes 8404997 | tf_op jit(solution)/shard_map/while/body/eval_jaxpr/dot_general | solution.py:42
  254.0 14.4 %fusion.11 = f32[256,3072]{1,0:T(8,128)S(1)} fusion(s32[4096]{0:T(1024)S(1)} %dynamic_slice.21, f32[256,3072]{1,0:T(8,128)S(1)} %get-tuple-element.142, bf16[16384,256]{1,0:T(8,128)(2,1)} %get-tuple-element.151, s32[]{:T(128)S(6)} %select_n.16, pred[]{:T(512)S(6)} %compare.3), kind=kOutput, calls=%fused_computation.3.clone.1 | convolution fusion | flops 6456606720 | bytes 8404997 | tf_op jit(solution)/shard_map/while/body/eval_jaxpr/dot_general | solution.py:42
  268.5 14.4 %fusion.11 = f32[256,3072]{1,0:T(8,128)S(1)} fusion(s32[4096]{0:T(1024)S(1)} %dynamic_slice.21, f32[256,3072]{1,0:T(8,128)S(1)} %get-tuple-element.142, bf16[16384,256]{1,0:T(8,128)(2,1)} %get-tuple-element.151, s32[]{:T(128)S(6)} %select_n.16, pred[]{:T(512)S(6)} %compare.3), kind=kOutput, calls=%fused_computation.3.clone.1 | convolution fusion | flops 6456606720 | bytes 8404997 | tf_op jit(solution)/shard_map/while/body/eval_jaxpr/dot_general | solution.py:42
  282.9 14.4 %fusion.11 = f32[256,3072]{1,0:T(8,128)S(1)} fusion(s32[4096]{0:T(1024)S(1)} %dynamic_slice.21, f32[256,3072]{1,0:T(8,128)S(1)} %get-tuple-element.142, bf16[16384,256]{1,0:T(8,128)(2,1)} %get-tuple-element.151, s32[]{:T(128)S(6)} %select_n.16, pred[]{:T(512)S(6)} %compare.3), kind=kOutput, calls=%fused_computation.3.clone.1 | convolution fusion | flops 6456606720 | bytes 8404997 | tf_op jit(solution)/shard_map/while/body/eval_jaxpr/dot_general | solution.py:42
  297.4 2.5 copy.15
  299.9 0.2 reduce_sum.54
  300.1 67.0 %all-gather = f32[98304]{0:T(1024)S(1)} all-gather(f32[3072]{0:T(1024)S(1)} %reduce_sum.54), channel_id=2, replica_groups=mesh['batch'=16,'gene'=2] {'batch','gene'}, dimensions={0}, use_global_device_ids=true | all-gather | bytes 405504 | tf_op jit(solution)/shard_map/all_gather | solution.py:50
  367.1 0.1 reshape.41
  367.2 3.1 divide_log-plus-one_fusion
  370.3 0.2 reduce_sum.56
  370.6 0.4 multiply_reduce_fusion
  371.0 1.6 fusion.5
  372.6 2.0 copy.16
  374.6 12.4 %multiply_convert_fusion = bf16[6144,2048]{1,0:T(8,128)(2,1)} fusion(bf16[6144,128]{1,0:T(8,128)(2,1)S(1)} %bitcast.21, bf16[128,2048]{1,0:T(8,128)(2,1)S(1)} %copy-done), kind=kOutput, calls=%fused_computation.6 | convolution fusion | flops 3246391296 | bytes 27262976 | tf_op jit(solution)/shard_map/dot_general | solution.py:60
  (20 shorter events, 0.2 us)
Async XLA Ops:
  16.5 8.3 %copy-start.2 = (s32[1024]{0:T(1024)S(1)}, s32[1024]{0:T(1024)}, u32[]{:S(2)}) copy-start(s32[1024]{0:T(1024)} %param.8) | copy-start | bytes 12292
  16.5 8.3 %copy-start.3 = (s32[1024]{0:T(1024)S(1)}, s32[1024]{0:T(1024)}, u32[]{:S(2)}) copy-start(s32[1024]{0:T(1024)} %param.9) | copy-start | bytes 12292
  16.5 159.5 %copy-start.1 = (s32[128,128]{1,0:T(8,128)S(1)}, s32[128,128]{1,0:T(8,128)}, u32[]{:S(2)}) copy-start(s32[128,128]{1,0:T(8,128)} %param.11) | copy-start | bytes 196612
  16.5 223.1 %all-to-all-start = ((bf16[1024,16,256]{2,0,1:T(8,128)(2,1)}), bf16[1024,16,256]{2,0,1:T(8,128)(2,1)}, u32[]{:S(2)}, u32[]{:S(2)}) async-start(bf16[1024,16,256]{2,0,1:T(8,128)(2,1)} %bitcast.20), calls=%async_computation | async-start | bytes 16777216 | tf_op jit(solution)/shard_map/all_to_all | solution.py:33
  372.6 2.0 copy-start
